TPU v7x, 32 devices: a whole 2x2x4 slice. The times are simulated.
32 devices in a mesh: pipe: 2 (over x), win: 4 (over y, core), fsdp: 4 (over z).
Axes of the slice: x: 2, y: 2, z: 4, core: 2. Of those that a mesh axis runs over, the one named last changes fastest.
Arguments:
- block_input: bfloat16 [64, 4, 49, 512], P('fsdp', 'win'), may hold values from -6 to 6
- out_grad: bfloat16 [64, 4, 49, 512], P('fsdp', 'win'), may hold values from -6 to 6
- norm_gains: bfloat16 [2, 2, 512], P('pipe', None, ('win', 'fsdp')), may hold values from 0.5 to 1.5
- norm_offsets: bfloat16 [2, 2, 512], P('pipe', None, ('win', 'fsdp')), may hold values from -2 to 2
- attend_weight: bfloat16 [2, 512, 1536], P('pipe', ('win', 'fsdp')), may hold values from -0.25 to 0.25
- row_biases: bfloat16 [2, 4, 512], P('pipe', None, ('win', 'fsdp')), may hold values from -2 to 2
- position_table: float32 [2, 169, 16], P('pipe'), may hold values from -2 to 302
- merge_weight: bfloat16 [2, 512, 512], P('pipe', ('win', 'fsdp')), may hold values from -0.5 to 0.5
- expand_weight: bfloat16 [2, 512, 2048], P('pipe', ('win', 'fsdp')), may hold values from -0.25 to 0.25
- hidden_biases: bfloat16 [2, 2048], P('pipe', ('win', 'fsdp')), may hold values from -2 to 2
- reduce_weight: bfloat16 [2, 2048, 512], P('pipe', ('win', 'fsdp')), may hold values from -0.125 to 0.125
- window_mask: int32 [4, 49, 49], P('win'), may hold values 0 or 1
- position_index: int32 [49, 49], replicated, may hold values from 0 to 168
Outputs:
- block_outputs: bfloat16 [2, 64, 4, 49, 512], P('pipe', 'fsdp', 'win')
- block_grads: float32 [2, 64, 4, 49, 512], P('pipe', 'fsdp', 'win')
- gain_grads: float32 [2, 2, 512], P('pipe', None, ('win', 'fsdp'))
- offset_grads: float32 [2, 2, 512], P('pipe', None, ('win', 'fsdp'))
- attend_grads: float32 [2, 512, 1536], P('pipe', ('win', 'fsdp'))
- bias_grads: float32 [2, 4, 512], P('pipe', None, ('win', 'fsdp'))
- table_grads: float32 [2, 169, 16], P('pipe')
- merge_grads: float32 [2, 512, 512], P('pipe', ('win', 'fsdp'))
- expand_grads: float32 [2, 512, 2048], P('pipe', ('win', 'fsdp'))
- hidden_grads: float32 [2, 2048], P('pipe', ('win', 'fsdp'))
- reduce_grads: float32 [2, 2048, 512], P('pipe', ('win', 'fsdp'))
All inputs are finite; a program needn't handle non-finite values. No bound on the sum of `window_mask` on one device may be relied on, other than what follows from the above.
Results may differ from a plain program's by a relative error of at most 0.022.
Values may be sent and summed in bfloat16 or wider, within the bound.
A program may use at most 256 MiB of HBM per device.

v0:
```python
import math

import jax
import jax.numpy as jnp
from jax import lax
from jax.sharding import PartitionSpec as P

norm_eps = 1e-05
mask_level = -100.0


def partner(block, axis, distance):
    count = lax.axis_size(axis)
    route = []
    for low in range(count):
        high = low | 1 << distance
        if high != low and high < count:
            route += [(low, high), (high, low)]
    return lax.ppermute(block, axis, route)


def from_behind(block, axis, distance):
    devices = range(lax.axis_size(axis))
    route = [(i - distance, i) for i in devices if i - distance in devices]
    return lax.ppermute(block, axis, route)


def matmul(operand, other):
    return jnp.dot(operand, other, preferred_element_type=jnp.float32)


def contract_rows(operand, other):
    return lax.dot_general(
        operand, other, (((0,), (0,)), ((), ())), preferred_element_type=jnp.float32
    )


def contract_cols(operand, other):
    return lax.dot_general(
        operand, other, (((1,), (1,)), ((), ())), preferred_element_type=jnp.float32
    )


def layer_norm(values, norm_gain, norm_offset):
    average = jnp.mean(values, axis=-1, keepdims=True)
    centered = values - average
    variance = jnp.mean(centered * centered, axis=-1, keepdims=True)
    inv_std = lax.rsqrt(variance + norm_eps)
    unit_rows = centered * inv_std
    return (unit_rows * norm_gain + norm_offset, unit_rows, inv_std)


def norm_back(d_normed, unit_rows, inv_std, norm_gain):
    d_unit = d_normed * norm_gain
    term_one = jnp.mean(d_unit, axis=-1, keepdims=True)
    term_two = jnp.mean(d_unit * unit_rows, axis=-1, keepdims=True)
    return inv_std * (d_unit - term_one - unit_rows * term_two)


def gaussian_gate(before):
    cumulative = 0.5 * (1.0 + jax.scipy.special.erf(before * (1.0 / math.sqrt(2.0))))
    density = jnp.exp(-0.5 * before * before) * (1.0 / math.sqrt(2.0 * math.pi))
    return (before * cumulative, cumulative + before * density)


def roll_ahead(windows):
    images = windows.shape[0]
    features = windows.shape[-1]
    side_cells = math.isqrt(windows.shape[2])
    window_grid = windows.reshape(images, side_cells, side_cells, features)
    upper_rows = partner(window_grid[:, :3], "win", 1)
    window_grid = jnp.concatenate([window_grid[:, 3:], upper_rows], axis=1)
    left_cols = partner(window_grid[:, :, :3], "win", 0)
    window_grid = jnp.concatenate([window_grid[:, :, 3:], left_cols], axis=2)
    return window_grid.reshape(windows.shape)


def roll_behind(windows):
    images = windows.shape[0]
    features = windows.shape[-1]
    side_cells = math.isqrt(windows.shape[2])
    window_grid = windows.reshape(images, side_cells, side_cells, features)
    lower_rows = partner(window_grid[:, side_cells - 3 :], "win", 1)
    window_grid = jnp.concatenate([lower_rows, window_grid[:, : side_cells - 3]], axis=1)
    right_cols = partner(window_grid[:, :, side_cells - 3 :], "win", 0)
    window_grid = jnp.concatenate([right_cols, window_grid[:, :, : side_cells - 3]], axis=2)
    return window_grid.reshape(windows.shape)


def attention_forward(rolled, attend_w, row_bias, bias_heads, mask_term):
    grid_shape = rolled.shape
    features = grid_shape[-1]
    head_count = bias_heads.shape[0]
    head_size = features // head_count
    score_scale = head_size ** (-0.5)
    projected = matmul(rolled.reshape(-1, features), attend_w)
    split_shape = grid_shape[:3] + (head_count, head_size)
    query_rows = (
        ((projected[:, :features] + row_bias[0]) * score_scale)
        .astype(jnp.bfloat16)
        .reshape(split_shape)
    )
    key_rows = projected[:, features : 2 * features].astype(jnp.bfloat16).reshape(split_shape)
    value_rows = (
        (projected[:, 2 * features :] + row_bias[1]).astype(jnp.bfloat16).reshape(split_shape)
    )
    scores = (
        jnp.einsum("bwihd,bwjhd->bwhij", query_rows, key_rows, preferred_element_type=jnp.float32)
        + bias_heads
        + mask_term[None, :, None]
    )
    row_max = jnp.max(scores, axis=-1, keepdims=True)
    log_total = row_max + jnp.log(jnp.sum(jnp.exp(scores - row_max), axis=-1, keepdims=True))
    weights = jnp.exp(scores - log_total).astype(jnp.bfloat16)
    attended = jnp.einsum(
        "bwhij,bwjhd->bwihd", weights, value_rows, preferred_element_type=jnp.float32
    )
    return (
        attended.reshape(grid_shape).astype(jnp.bfloat16),
        query_rows,
        key_rows,
        value_rows,
        log_total,
    )


def attention_backward(
    d_attended, query_rows, key_rows, value_rows, log_total, bias_heads, mask_term
):
    features = d_attended.shape[-1]
    head_size = query_rows.shape[-1]
    score_scale = head_size ** (-0.5)
    scores = (
        jnp.einsum("bwihd,bwjhd->bwhij", query_rows, key_rows, preferred_element_type=jnp.float32)
        + bias_heads
        + mask_term[None, :, None]
    )
    probs = jnp.exp(scores - log_total)
    d_att = d_attended.reshape(query_rows.shape)
    d_value = jnp.einsum(
        "bwhij,bwihd->bwjhd", probs.astype(jnp.bfloat16), d_att, preferred_element_type=jnp.float32
    )
    d_probs = jnp.einsum(
        "bwihd,bwjhd->bwhij", d_att, value_rows, preferred_element_type=jnp.float32
    )
    d_scores = probs * (d_probs - jnp.sum(probs * d_probs, axis=-1, keepdims=True))
    d_bias = jnp.sum(d_scores, axis=(0, 1))
    scores_half = d_scores.astype(jnp.bfloat16)
    d_query = (
        jnp.einsum("bwhij,bwjhd->bwihd", scores_half, key_rows, preferred_element_type=jnp.float32)
        * score_scale
    )
    d_key = jnp.einsum(
        "bwhij,bwihd->bwjhd", scores_half, query_rows, preferred_element_type=jnp.float32
    )
    d_query = d_query.reshape(-1, features)
    d_key = d_key.reshape(-1, features)
    d_value = d_value.reshape(-1, features)
    d_proj = jnp.concatenate([d_query, d_key, d_value], axis=1).astype(jnp.bfloat16)
    return (d_proj, d_bias, jnp.sum(d_query, axis=0), jnp.sum(d_value, axis=0))


def block_forward(inputs, params, ahead, behind, bias_heads, mask_term):
    gains, offsets, attend_w, row_bias, merge_w, expand_w, hidden_bias, reduce_w = params
    grid_shape = inputs.shape
    features = grid_shape[-1]
    inputs_flat = inputs.reshape(-1, features)
    normed_one = layer_norm(inputs_flat, gains[0], offsets[0])[0].astype(jnp.bfloat16)
    rolled = ahead(normed_one.reshape(grid_shape))
    attended, query_rows, key_rows, value_rows, log_total = attention_forward(
        rolled, attend_w, row_bias, bias_heads, mask_term
    )
    unrolled = behind(attended)
    middle = inputs_flat + matmul(unrolled.reshape(-1, features), merge_w) + row_bias[2]
    normed_two = layer_norm(middle, gains[1], offsets[1])[0].astype(jnp.bfloat16)
    before = matmul(normed_two, expand_w) + hidden_bias
    hidden = gaussian_gate(before)[0].astype(jnp.bfloat16)
    outputs = middle + matmul(hidden, reduce_w) + row_bias[3]
    retained = (
        inputs_flat,
        rolled,
        query_rows,
        key_rows,
        value_rows,
        log_total,
        unrolled,
        middle,
        normed_two,
        before,
    )
    return (outputs.reshape(grid_shape), retained)


def block_backward(cotangent, retained, params, ahead, behind, bias_heads, mask_term):
    gains, offsets, attend_w, row_bias, merge_w, expand_w, hidden_bias, reduce_w = params
    (
        inputs_flat,
        rolled,
        query_rows,
        key_rows,
        value_rows,
        log_total,
        unrolled,
        middle,
        normed_two,
        before,
    ) = retained
    grid_shape = cotangent.shape
    features = grid_shape[-1]
    cot_flat = cotangent.reshape(-1, features)
    active, gate_slope = gaussian_gate(before)
    hidden = active.astype(jnp.bfloat16)
    reduce_g = contract_rows(hidden, cot_flat)
    bias_three = jnp.sum(cot_flat.astype(jnp.float32), axis=0)
    d_before = (contract_cols(cot_flat, reduce_w) * gate_slope).astype(jnp.bfloat16)
    expand_g = contract_rows(normed_two, d_before)
    hidden_g = jnp.sum(d_before.astype(jnp.float32), axis=0)
    d_normed_two = contract_cols(d_before, expand_w)
    unit_two, inv_two = layer_norm(middle, gains[1], offsets[1])[1:]
    gain_two = jnp.sum(d_normed_two * unit_two, axis=0)
    offset_two = jnp.sum(d_normed_two, axis=0)
    d_middle = cot_flat.astype(jnp.float32) + norm_back(d_normed_two, unit_two, inv_two, gains[1])
    d_branch = d_middle.astype(jnp.bfloat16)
    merge_g = contract_rows(unrolled.reshape(-1, features), d_branch)
    bias_two = jnp.sum(d_middle, axis=0)
    d_unrolled = contract_cols(d_branch, merge_w).astype(jnp.bfloat16).reshape(grid_shape)
    d_attended = ahead(d_unrolled)
    d_proj, d_bias, query_g, value_g = attention_backward(
        d_attended, query_rows, key_rows, value_rows, log_total, bias_heads, mask_term
    )
    attend_g = contract_rows(rolled.reshape(-1, features), d_proj)
    d_rolled = contract_cols(d_proj, attend_w).astype(jnp.bfloat16).reshape(grid_shape)
    d_normed_one = behind(d_rolled).reshape(-1, features).astype(jnp.float32)
    unit_one, inv_one = layer_norm(inputs_flat, gains[0], offsets[0])[1:]
    gain_one = jnp.sum(d_normed_one * unit_one, axis=0)
    offset_one = jnp.sum(d_normed_one, axis=0)
    d_inputs = d_middle + norm_back(d_normed_one, unit_one, inv_one, gains[0])
    gradients = (
        jnp.stack([gain_one, gain_two]),
        jnp.stack([offset_one, offset_two]),
        attend_g,
        jnp.stack([query_g, value_g, bias_two, bias_three]),
        d_bias,
        merge_g,
        expand_g,
        hidden_g,
        reduce_g,
    )
    return (d_inputs.reshape(grid_shape), gradients)


def widen_params(gathered):
    f32 = jnp.float32
    return (
        gathered[0].astype(f32),
        gathered[1].astype(f32),
        gathered[2],
        gathered[3].astype(f32),
        gathered[4],
        gathered[5],
        gathered[6].astype(f32),
        gathered[7],
    )


def shards(
    block_input,
    out_grad,
    norm_gains,
    norm_offsets,
    attend_weight,
    row_biases,
    position_table,
    merge_weight,
    expand_weight,
    hidden_biases,
    reduce_weight,
    window_mask,
    position_index,
):
    section_index = lax.axis_index("pipe")
    shifted = section_index == 1
    head_count = position_table.shape[-1]
    table_rows = position_table.shape[1]
    local_shard = (
        norm_gains[0],
        norm_offsets[0],
        attend_weight[0],
        row_biases[0],
        merge_weight[0],
        expand_weight[0],
        hidden_biases[0],
        reduce_weight[0],
    )
    gathered = (
        lax.all_gather(local_shard[0], ("win", "fsdp"), axis=1, tiled=True),
        lax.all_gather(local_shard[1], ("win", "fsdp"), axis=1, tiled=True),
        lax.all_gather(local_shard[2], ("win", "fsdp"), axis=0, tiled=True),
        lax.all_gather(local_shard[3], ("win", "fsdp"), axis=1, tiled=True),
        lax.all_gather(local_shard[4], ("win", "fsdp"), axis=0, tiled=True),
        lax.all_gather(local_shard[5], ("win", "fsdp"), axis=0, tiled=True),
        lax.all_gather(local_shard[6], ("win", "fsdp"), axis=0, tiled=True),
        lax.all_gather(local_shard[7], ("win", "fsdp"), axis=0, tiled=True),
    )
    params = widen_params(gathered)
    window_cells = position_index.shape[0]
    one_hot = (
        position_index.reshape(-1)[:, None] == jnp.arange(table_rows, dtype=jnp.int32)[None, :]
    ).astype(jnp.float32)
    bias_flat = jnp.dot(one_hot, position_table[0], precision=lax.Precision.HIGHEST)
    bias_heads = bias_flat.reshape(window_cells, window_cells, head_count).transpose(2, 0, 1)
    mask_term = jnp.where(shifted, mask_level * window_mask.astype(jnp.float32), 0.0)

    def ahead(values):
        return jnp.where(shifted, roll_ahead(values), values)

    def behind(values):
        return jnp.where(shifted, roll_behind(values), values)

    part_count = 1
    per_part = block_input.shape[0] // part_count
    received = jnp.zeros((per_part,) + block_input.shape[1:], jnp.bfloat16)
    stored = []
    produced = []
    for tick_index in range(part_count + 1):
        section_feed = jnp.where(shifted, received, block_input).astype(jnp.float32)
        result, retained = block_forward(section_feed, params, ahead, behind, bias_heads, mask_term)
        result_half = result.astype(jnp.bfloat16)
        stored.append(retained)
        produced.append(result_half)
        if tick_index < part_count:
            received = from_behind(result_half, "pipe", 1)
    block_outputs = jnp.where(
        shifted,
        jnp.concatenate(produced[1:], axis=0),
        jnp.concatenate(produced[:part_count], axis=0),
    )
    regathered = (
        lax.all_gather(local_shard[0], ("win", "fsdp"), axis=1, tiled=True),
        lax.all_gather(local_shard[1], ("win", "fsdp"), axis=1, tiled=True),
        lax.all_gather(local_shard[2], ("win", "fsdp"), axis=0, tiled=True),
        lax.all_gather(local_shard[3], ("win", "fsdp"), axis=1, tiled=True),
        lax.all_gather(local_shard[4], ("win", "fsdp"), axis=0, tiled=True),
        lax.all_gather(local_shard[5], ("win", "fsdp"), axis=0, tiled=True),
        lax.all_gather(local_shard[6], ("win", "fsdp"), axis=0, tiled=True),
        lax.all_gather(local_shard[7], ("win", "fsdp"), axis=0, tiled=True),
    )
    back_params = widen_params(regathered)
    back_received = jnp.zeros((per_part,) + block_input.shape[1:], jnp.bfloat16)
    running = None
    d_list = []
    for tick_index in range(part_count + 1):
        cotangent = jnp.where(shifted, out_grad, back_received)
        retained = jax.tree.map(
            lambda latest, earlier: jnp.where(shifted, latest, earlier),
            stored[min(tick_index + 1, part_count)],
            stored[max(tick_index - 1, 0)],
        )
        d_inputs, gradients = block_backward(
            cotangent, retained, back_params, ahead, behind, bias_heads, mask_term
        )
        valid_flag = jnp.where(shifted, tick_index < part_count, tick_index >= 1)
        masked = jax.tree.map(lambda update: jnp.where(valid_flag, update, 0.0), gradients)
        if running is None:
            running = masked
        else:
            running = jax.tree.map(lambda earlier, update: earlier + update, running, masked)
        d_list.append(d_inputs)
        if tick_index < part_count:
            back_received = from_behind(d_inputs.astype(jnp.bfloat16), "pipe", -1)
    block_grads = jnp.where(
        shifted, jnp.concatenate(d_list[:part_count], axis=0), jnp.concatenate(d_list[1:], axis=0)
    )
    table_local = jnp.dot(
        one_hot.T,
        running[4].transpose(1, 2, 0).reshape(-1, head_count),
        precision=lax.Precision.HIGHEST,
    )
    table_grads = lax.psum(table_local, ("win", "fsdp"))
    shares = (
        lax.psum_scatter(running[0], ("win", "fsdp"), scatter_dimension=1, tiled=True),
        lax.psum_scatter(running[1], ("win", "fsdp"), scatter_dimension=1, tiled=True),
        lax.psum_scatter(running[2], ("win", "fsdp"), scatter_dimension=0, tiled=True),
        lax.psum_scatter(running[3], ("win", "fsdp"), scatter_dimension=1, tiled=True),
        lax.psum_scatter(running[5], ("win", "fsdp"), scatter_dimension=0, tiled=True),
        lax.psum_scatter(running[6], ("win", "fsdp"), scatter_dimension=0, tiled=True),
        lax.psum_scatter(running[7], ("win", "fsdp"), scatter_dimension=0, tiled=True),
        lax.psum_scatter(running[8], ("win", "fsdp"), scatter_dimension=0, tiled=True),
    )
    return (
        block_outputs[None],
        block_grads[None],
        shares[0][None],
        shares[1][None],
        shares[2][None],
        shares[3][None],
        table_grads[None],
        shares[4][None],
        shares[5][None],
        shares[6][None],
        shares[7][None],
    )


def solution(mesh):
    placed = (
        P("fsdp", "win", None, None),
        P("fsdp", "win", None, None),
        P("pipe", None, ("win", "fsdp")),
        P("pipe", None, ("win", "fsdp")),
        P("pipe", ("win", "fsdp"), None),
        P("pipe", None, ("win", "fsdp")),
        P("pipe", None, None),
        P("pipe", ("win", "fsdp"), None),
        P("pipe", ("win", "fsdp"), None),
        P("pipe", ("win", "fsdp")),
        P("pipe", ("win", "fsdp"), None),
        P("win", None, None),
        P(),
    )
    return jax.shard_map(
        shards,
        mesh=mesh,
        in_specs=placed,
        out_specs=(
            P("pipe", "fsdp", "win", None, None),
            P("pipe", "fsdp", "win", None, None),
            P("pipe", None, ("win", "fsdp")),
            P("pipe", None, ("win", "fsdp")),
            P("pipe", ("win", "fsdp"), None),
            P("pipe", None, ("win", "fsdp")),
            P("pipe", None, None),
            P("pipe", ("win", "fsdp"), None),
            P("pipe", ("win", "fsdp"), None),
            P("pipe", ("win", "fsdp")),
            P("pipe", ("win", "fsdp"), None),
        ),
        check_vma=False,
    )
```

profile of v0, /device:TPU:0, one launch (start us, length us, event | category | flops | bytes accessed | tf_op | source)
XLA Modules:
  0.0 1198.6 jit_solution(17671154045653519769)
XLA Ops:
  9.5 37.1 %all-gather.1 = bf16[1,2,512]{1,0,2:T(2,128)(2,1)S(1)} all-gather(bf16[1,2,32]{1,0,2:T(2,128)(2,1)S(1)} %copy.277), channel_id=3, replica_groups=mesh['pipe'=2,'win'=4,'fsdp'=4] {'win','fsdp'}, dimensions={2}, use_global_device_ids=true | all-gather | bytes 2176 | tf_op jit(solution)/shard_map/all_gather | solution.py:297
  47.6 31.0 %all-gather = bf16[1,2,512]{1,0,2:T(2,128)(2,1)S(1)} all-gather(bf16[1,2,32]{1,0,2:T(2,128)(2,1)S(1)} %copy.276), channel_id=2, replica_groups=mesh['pipe'=2,'win'=4,'fsdp'=4] {'win','fsdp'}, dimensions={2}, use_global_device_ids=true | all-gather | bytes 2176 | tf_op jit(solution)/shard_map/all_gather | solution.py:296
  89.9 4.8 collective-permute-done
  95.5 35.8 %all-gather.3 = bf16[1,4,512]{1,0,2:T(2,128)(2,1)S(1)} all-gather(bf16[1,4,32]{1,0,2:T(2,128)(2,1)S(1)} %copy.279), channel_id=5, replica_groups=mesh['pipe'=2,'win'=4,'fsdp'=4] {'win','fsdp'}, dimensions={2}, use_global_device_ids=true | all-gather | bytes 4352 | tf_op jit(solution)/shard_map/all_gather | solution.py:299
  132.0 6.7 slice_reduce_fusion
  161.6 7.4 fusion.4
  171.3 5.9 reshape.822
  177.2 5.6 exponential_reduce_fusion.1
  186.9 6.9 copy.289
  200.9 5.2 collective-permute-done.2
  211.5 28.5 %all-gather.6 = bf16[1,2048]{1,0:T(2,128)(2,1)S(1)} all-gather(bf16[1,128]{1,0:T(2,128)(2,1)S(1)} %copy-done.101), channel_id=8, replica_groups=mesh['pipe'=2,'win'=4,'fsdp'=4] {'win','fsdp'}, dimensions={1}, use_global_device_ids=true | all-gather | bytes 4352 | tf_op jit(solution)/shard_map/all_gather | solution.py:302
  240.0 38.3 %all-gather.4 = bf16[1,512,512]{2,1,0:T(8,128)(2,1)} all-gather(bf16[1,32,512]{2,1,0:T(8,128)(2,1)S(1)} %copy-done.86), channel_id=6, replica_groups=mesh['pipe'=2,'win'=4,'fsdp'=4] {'win','fsdp'}, dimensions={1}, use_global_device_ids=true | all-gather | bytes 557056 | tf_op jit(solution)/shard_map/all_gather | solution.py:300
  282.4 5.4 reshape.879
  292.9 6.3 fusion.41
  299.3 5.4 add_convert_fusion.4
  309.6 13.6 %collective-permute-done.4 = bf16[16,1,49,512]{3,0,2,1:T(8,128)(2,1)S(1)} collective-permute-done((bf16[16,1,49,512]{3,0,2,1:T(8,128)(2,1)S(1)}, bf16[16,1,49,512]{3,0,2,1:T(8,128)(2,1)S(1)}, u32[]{:S(2)}, u32[]{:S(2)}) %collective-permute-start.4) | collective-permute-done | bytes 802848 | tf_op jit(solution)/shard_map/ppermute | solution.py:25
  326.9 6.4 collective-permute-done.5
  353.1 5.1 fusion.5
  366.8 7.5 convert_bitcast_fusion.2
  374.2 7.6 copy.303
  387.5 9.2 collective-permute-done.7
  403.6 5.7 copy.356
  409.3 5.5 reshape.880
  424.5 7.3 multiply_convert_fusion
  431.8 4.9 convert_reduce_fusion.1
  444.7 9.7 collective-permute-done.9
  461.3 5.5 reshape.836
  471.7 5.5 copy.313
  488.4 9.1 fusion.21
  497.5 6.4 bitcast_convert_fusion.3
  507.3 5.0 bitcast_convert_fusion.2
  544.4 10.7 collective-permute-done.11
  571.0 20.8 %collective-permute-done.13 = bf16[16,1,49,512]{3,0,2,1:T(8,128)(2,1)} collective-permute-done((bf16[16,1,49,512]{3,0,2,1:T(8,128)(2,1)}, bf16[16,1,49,512]{3,0,2,1:T(8,128)(2,1)}, u32[]{:S(2)}, u32[]{:S(2)}) %collective-permute-start.13) | collective-permute-done | bytes 802848 | tf_op jit(solution)/shard_map/ppermute | solution.py:25
  597.0 6.3 convert_reduce_fusion
  616.6 6.1 collective-permute-done.14
  626.2 5.4 reshape.843
  635.6 4.8 reshape.882
  640.4 5.7 copy.330
  648.1 10.8 multiply_reduce_fusion
  659.0 6.7 fusion.20
  672.7 4.7 bitcast_convert_fusion
  778.5 5.6 fusion.114
  792.7 64.1 %all-reduce.1 = (f32[1,169,16]{1,2,0:T(8,128)}, f32[2048]{0:T(1024)S(1)}) all-reduce(f32[1,169,16]{1,2,0:T(8,128)S(1)} %fusion.120, f32[2048]{0:T(1024)S(1)} %select_add_fusion.2), channel_id=1, replica_groups=mesh['pipe'=2,'win'=4,'fsdp'=4] {'win','fsdp'}, use_global_device_ids=true, to_apply=%region_48.49 | all-reduce | flops 4752 | bytes 38016 | tf_op jit(solution)/shard_map/psum | solution.py:379
  867.4 40.7 %reduce-scatter.24.cloned.1.call-done = f32[32,2]{1,0:T(8,128)} async-done(((f32[512,2]{1,0:T(8,128)}), f32[32,2]{1,0:T(8,128)}) %reduce-scatter.24.cloned.1.call-update) | async-done | bytes 272
  909.5 59.5 %reduce-scatter.16.cloned.1.call-done = f32[32,512]{1,0:T(8,128)} async-done(((f32[512,512]{1,0:T(8,128)}), f32[32,512]{1,0:T(8,128)}) %reduce-scatter.16.cloned.1.call-update) | async-done | bytes 65552 | tf_op jit(solution)/shard_map/reduce_scatter | solution.py:385
  969.0 69.7 %reduce-scatter.14.cloned.1.call-done = f32[32,1536]{1,0:T(8,128)} async-done(((f32[512,1536]{1,0:T(8,128)}), f32[32,1536]{1,0:T(8,128)}) %reduce-scatter.14.cloned.1.call-update) | async-done | bytes 196624 | tf_op jit(solution)/shard_map/reduce_scatter | solution.py:383
  1038.7 76.3 %reduce-scatter.18.cloned.1.call-done = f32[32,2048]{1,0:T(8,128)} async-done(((f32[512,2048]{1,0:T(8,128)}), f32[32,2048]{1,0:T(8,128)}) %reduce-scatter.18.cloned.1.call-update) | async-done | bytes 262160 | tf_op jit(solution)/shard_map/reduce_scatter | solution.py:386
  1115.0 76.3 %reduce-scatter.20.cloned.1.call-done = f32[128,512]{1,0:T(8,128)} async-done(((f32[2048,512]{1,0:T(8,128)}), f32[128,512]{1,0:T(8,128)}) %reduce-scatter.20.cloned.1.call-update) | async-done | bytes 262160 | tf_op jit(solution)/shard_map/reduce_scatter | solution.py:388
  (509 shorter events, 363.2 us)
Async XLA Ops:
  7.2 80.8 %copy-start = (f32[1,169,16]{1,2,0:T(8,128)S(1)}, f32[1,169,16]{1,2,0:T(8,128)}, u32[]{:S(2)}) copy-start(f32[1,169,16]{1,2,0:T(8,128)} %param.19) | copy-start | bytes 32452
  7.2 71.7 %copy-start.14 = (bf16[16,1,49,512]{3,0,2,1:T(8,128)(2,1)S(1)}, bf16[16,1,49,512]{3,0,2,1:T(8,128)(2,1)}, u32[]{:S(2)}) copy-start(bf16[16,1,49,512]{3,0,2,1:T(8,128)(2,1)} %param.13) | copy-start | bytes 2408452
  7.2 134.8 %all-gather.12.cloned.1.call-start = ((), (), s32[]{:S(2)}) async-start(), calls=%async_computation.11 | async-start | bytes 1671168 | tf_op jit(solution)/shard_map/all_gather | solution.py:298
  7.9 284.9 %all-gather.14.cloned.1.call-start = ((), (), s32[]{:S(2)}) async-start(), calls=%async_computation.12 | async-start | bytes 2228224 | tf_op jit(solution)/shard_map/all_gather | solution.py:301
  8.7 290.6 %all-gather.16.cloned.1.call-start = ((), (), s32[]{:S(2)}) async-start(), calls=%async_computation.13 | async-start | bytes 2228224 | tf_op jit(solution)/shard_map/all_gather | solution.py:303
  82.3 57.5 %copy-start.82 = (f32[512]{0:T(512)}, f32[512]{0:T(512)S(1)}, u32[]{:S(2)}) copy-start(f32[512]{0:T(512)S(1)} %get-tuple-element.93) | copy-start | bytes 6148
  82.3 210.6 %copy-start.79 = (f32[512]{0:T(512)}, f32[512]{0:T(512)S(1)}, u32[]{:S(2)}) copy-start(f32[512]{0:T(512)S(1)} %get-tuple-element.92) | copy-start | bytes 6148
  86.7 8.0 collective-permute-start
  87.7 769.7 %reduce-scatter.26.cloned.1.call-start = ((), (), s32[]{:S(2)}) async-start(), calls=%async_computation.16 | async-start | bytes 278528
  95.5 43.3 %collective-permute-start.1 = (bf16[16,7,3,512]{3,0,2,1:T(8,128)(2,1)}, bf16[16,7,3,512]{3,0,2,1:T(8,128)(2,1)}, u32[]{:S(2)}, u32[]{:S(2)}) collective-permute-start(bf16[16,7,3,512]{3,0,2,1:T(8,128)(2,1)} %pad_maximum_fusion.13), channel_id=1, source_target_pairs={{0,4},{4,0},{8,12},{12,8},{1,5},{5,1},{9,13},{13,9},{2,6},{6,2},{1... | collective-permute-start | bytes 1032200 | tf_op jit(solution)/shard_map/ppermute | solution.py:19
  131.9 29.6 %copy-start.11 = (f32[16,49,49]{1,2,0:T(8,128)}, f32[16,49,49]{1,2,0:T(8,128)S(1)}, u32[]{:S(2)}) copy-start(f32[16,49,49]{1,2,0:T(8,128)S(1)} %copy.285) | copy-start | bytes 460996
  138.7 151.8 %copy-start.90 = (f32[512]{0:T(512)}, f32[512]{0:T(512)S(1)}, u32[]{:S(2)}) copy-start(f32[512]{0:T(512)S(1)} %get-tuple-element.87) | copy-start | bytes 6148
  138.7 160.6 %copy-start.98 = (f32[512]{0:T(512)}, f32[512]{0:T(512)S(1)}, u32[]{:S(2)}) copy-start(f32[512]{0:T(512)S(1)} %get-tuple-element.86) | copy-start | bytes 6148
  169.0 13.9 %slice-start.4 = ((s8[7340032]{0:T(1024)(128)(4,1)}), s8[3145728]{0:T(1024)(128)(4,1)S(1)}, s32[]{:S(2)}) async-start(s8[7340032]{0:T(1024)(128)(4,1)} %bitcast.259), calls=%async_computation.21 | async-start | bytes 6291456
  198.8 7.3 collective-permute-start.2
  206.1 81.7 %collective-permute-start.3 = (bf16[16,7,3,512]{3,0,2,1:T(8,128)(2,1)S(1)}, bf16[16,7,3,512]{3,0,2,1:T(8,128)(2,1)}, u32[]{:S(2)}, u32[]{:S(2)}) collective-permute-start(bf16[16,7,3,512]{3,0,2,1:T(8,128)(2,1)S(1)} %pad_maximum_fusion.12), channel_id=1, source_target_pairs={{0,4},{4,0},{8,12},{12,8},{1,5},{5,1},{9,13},{13,9},{2,6},{6,2},{1... | collective-permute-start | bytes 1032200 | tf_op jit(solution)/shard_map/ppermute | solution.py:19
  208.4 31.5 %copy-start.86 = (bf16[1,32,512]{2,1,0:T(8,128)(2,1)S(1)}, bf16[1,32,512]{2,1,0:T(8,128)(2,1)}, u32[]{:S(2)}) copy-start(bf16[1,32,512]{2,1,0:T(8,128)(2,1)} %param.20) | copy-start | bytes 98308
  208.4 69.8 %copy-start.32 = (bf16[16,1,49,16,32]{2,4,3,0,1:T(8,128)(2,1)S(1)}, bf16[16,1,49,16,32]{2,4,3,0,1:T(8,128)(2,1)}, u32[]{:S(2)}) copy-start(bf16[16,1,49,16,32]{2,4,3,0,1:T(8,128)(2,1)} %convert_bitcast_fusion.3) | copy-start | bytes 2408452
  240.0 183.8 %copy-start.84 = (f32[1,2048]{1,0:T(1,128)}, f32[1,2048]{1,0:T(1,128)S(1)}, u32[]{:S(2)}) copy-start(f32[1,2048]{1,0:T(1,128)S(1)} %convert_element_type.301) | copy-start | bytes 24580
  304.6 18.6 %copy-start.15 = (bf16[16,1,49,512]{3,0,2,1:T(8,128)(2,1)S(1)}, bf16[16,1,49,512]{3,0,2,1:T(8,128)(2,1)}, u32[]{:S(2)}) copy-start(bf16[16,1,49,512]{3,0,2,1:T(8,128)(2,1)} %param.13) | copy-start | bytes 2408452
  306.4 16.9 %collective-permute-start.4 = (bf16[16,1,49,512]{3,0,2,1:T(8,128)(2,1)S(1)}, bf16[16,1,49,512]{3,0,2,1:T(8,128)(2,1)S(1)}, u32[]{:S(2)}, u32[]{:S(2)}) collective-permute-start(bf16[16,1,49,512]{3,0,2,1:T(8,128)(2,1)S(1)} %copy.293), channel_id=1, source_target_pairs={{0,16},{1,17},{2,18},{3,19},{4,20},{5,21},{6,22},{7,23},{8,24},{9,... | collective-permute-start | bytes 2408456 | tf_op jit(solution)/shard_map/ppermute | solution.py:25
  325.9 7.3 collective-permute-start.5
  333.3 1.7 collective-permute-start.6
  386.6 10.2 collective-permute-start.7
  397.6 17.2 %collective-permute-start.8 = (bf16[16,7,3,512]{3,0,2,1:T(8,128)(2,1)}, bf16[16,7,3,512]{3,0,2,1:T(8,128)(2,1)}, u32[]{:S(2)}, u32[]{:S(2)}) collective-permute-start(bf16[16,7,3,512]{3,0,2,1:T(8,128)(2,1)} %pad_maximum_fusion.10), channel_id=1, source_target_pairs={{0,4},{4,0},{8,12},{12,8},{1,5},{5,1},{9,13},{13,9},{2,6},{6,2},{1... | collective-permute-start | bytes 1032200 | tf_op jit(solution)/shard_map/ppermute | solution.py:19
  403.6 15.0 %copy-start.39 = (f32[784,512]{1,0:T(8,128)}, f32[784,512]{1,0:T(8,128)S(1)}, u32[]{:S(2)}) copy-start(f32[784,512]{1,0:T(8,128)S(1)} %reshape.826) | copy-start | bytes 4816900
  423.4 15.7 %copy-start.22 = (f32[784,512]{1,0:T(8,128)}, f32[784,512]{1,0:T(8,128)S(1)}, u32[]{:S(2)}) copy-start(f32[784,512]{1,0:T(8,128)S(1)} %get-tuple-element.114) | copy-start | bytes 4816900
  441.6 14.5 %copy-start.28 = (bf16[16,49,16,32]{1,0,3,2:T(8,128)(2,1)S(1)}, bf16[16,49,16,32]{1,0,3,2:T(8,128)(2,1)}, u32[]{:S(2)}) copy-start(bf16[16,49,16,32]{1,0,3,2:T(8,128)(2,1)} %copy-done.27) | copy-start | bytes 2408452
  442.7 11.6 collective-permute-start.9
  456.1 11.2 collective-permute-start.10
  488.4 18.9 %copy-start.2 = (f32[16,16,49,49]{2,3,1,0:T(8,128)}, f32[16,16,49,49]{2,3,1,0:T(8,128)S(1)}, u32[]{:S(2)}) copy-start(f32[16,16,49,49]{2,3,1,0:T(8,128)S(1)} %get-tuple-element.134) | copy-start | bytes 7375876
  541.8 13.7 %copy-start.76 = (f32[16,49]{0,1:T(8,128)S(1)}, f32[16,49]{0,1:T(8,128)}, u32[]{:S(2)}) copy-start(f32[16,49]{0,1:T(8,128)} %get-tuple-element.84) | copy-start | bytes 9412
  543.4 11.6 collective-permute-start.11
  555.4 2.0 collective-permute-start.12
  562.8 176.1 %copy-start.19 = (f32[784,512]{1,0:T(8,128)}, f32[784,512]{1,0:T(8,128)S(1)}, u32[]{:S(2)}) copy-start(f32[784,512]{1,0:T(8,128)S(1)} %get-tuple-element.110) | copy-start | bytes 4816900
  569.7 22.1 %collective-permute-start.13 = (bf16[16,1,49,512]{3,0,2,1:T(8,128)(2,1)}, bf16[16,1,49,512]{3,0,2,1:T(8,128)(2,1)}, u32[]{:S(2)}, u32[]{:S(2)}) collective-permute-start(bf16[16,1,49,512]{3,0,2,1:T(8,128)(2,1)} %copy.326), channel_id=1, source_target_pairs={{16,0},{17,1},{18,2},{19,3},{20,4},{21,5},{22,6},{23,7},{24,8},{25... | collective-permute-start | bytes 2408456 | tf_op jit(solution)/shard_map/ppermute | solution.py:25
  612.3 10.4 collective-permute-start.14
  623.6 9.6 collective-permute-start.15
  715.9 11.8 collective-permute-start.16
  730.1 4.0 collective-permute-start.17
  733.8 132.3 %reduce-scatter.22.cloned.1.call-start = ((), (), s32[]{:S(2)}) async-start(), calls=%async_computation.14 | async-start | bytes 278528
  742.5 165.6 %reduce-scatter.24.cloned.1.call-start = ((), (), s32[]{:S(2)}) async-start(), calls=%async_computation.15 | async-start | bytes 278528
  743.5 225.4 %reduce-scatter.16.cloned.1.call-start = ((), (), s32[]{:S(2)}) async-start(), calls=%async_computation.8 | async-start | bytes 1114112 | tf_op jit(solution)/shard_map/reduce_scatter | solution.py:385
  747.3 291.3 %reduce-scatter.14.cloned.1.call-start = ((), (), s32[]{:S(2)}) async-start(), calls=%async_computation.7 | async-start | bytes 3342336 | tf_op jit(solution)/shard_map/reduce_scatter | solution.py:383
  755.6 359.4 %reduce-scatter.18.cloned.1.call-start = ((), (), s32[]{:S(2)}) async-start(), calls=%async_computation.9 | async-start | bytes 4456448 | tf_op jit(solution)/shard_map/reduce_scatter | solution.py:386
  766.3 425.0 %reduce-scatter.20.cloned.1.call-start = ((), (), s32[]{:S(2)}) async-start(), calls=%async_computation.10 | async-start | bytes 4456448 | tf_op jit(solution)/shard_map/reduce_scatter | solution.py:388
  786.6 72.2 %copy-start.20 = (f32[784,512]{1,0:T(8,128)S(1)}, f32[784,512]{1,0:T(8,128)}, u32[]{:S(2)}) copy-start(f32[784,512]{1,0:T(8,128)} %copy-done.19) | copy-start | bytes 4816900
  858.8 332.5 %copy-start.1 = (f32[1,169,16]{1,2,0:T(8,128)S(1)}, f32[1,169,16]{1,2,0:T(8,128)}, u32[]{:S(2)}) copy-start(f32[1,169,16]{1,2,0:T(8,128)} %param.19) | copy-start | bytes 32452
  (94 other events, 421.7 us)
Sparse Core Ops, SparseCore 0:
  10.3 42.8 all-gather.11
  55.4 40.8 all-gather.13
  98.6 41.3 all-gather.15
  733.9 57.7 reduce-scatter.25
  795.1 54.7 reduce-scatter.21
  853.3 54.7 reduce-scatter.23
  912.3 56.5 reduce-scatter.15
  973.3 65.3 reduce-scatter.13
  1043.1 71.8 reduce-scatter.17
  1119.3 71.9 reduce-scatter.19
where the time goes:
time: 1210 us; the launch traced here: 1200 us
  waiting for transfers between devices  417 us (34%)
  local copies, waits for them, and re-layouts  262 us (22%)
  blocking collectives  235 us (19%)
  matrix products  162 us (13%)
  other arithmetic  92.9 us (8%)
  between operations  17.2 us (1%)
  starting transfers between devices  12.9 us (1%)
    reduce_scatter x1, waiting for transfers between devices, shards(): lax.psum_scatter(running[6], ('win', 'fsdp'), scatter_dimension=0, tiled=...  76.3 us
    reduce_scatter x1, waiting for transfers between devices, shards(): lax.psum_scatter(running[8], ('win', 'fsdp'), scatter_dimension=0, tiled=...  76.3 us
    reduce_scatter x1, waiting for transfers between devices, shards(): lax.psum_scatter(running[2], ('win', 'fsdp'), scatter_dimension=0, tiled=...  69.7 us
    psum x1, blocking collectives, shards(): table_grads = lax.psum(table_local, ('win', 'fsdp'))  64.1 us
    reduce_scatter x1, waiting for transfers between devices, shards(): lax.psum_scatter(running[5], ('win', 'fsdp'), scatter_dimension=0, tiled=...  59.5 us
    ppermute x16, waiting for transfers between devices, partner(): return lax.ppermute(block, axis, route)  58.8 us
    convert_element_type x8, local copies, waits for them, and re-layouts, attention_forward(): attended.reshape(grid_shape).astype(jnp.bfloat16)  43.7 us
    unnamed x13, waiting for transfers between devices  42.2 us
  transfers between devices with their start and end apart: 28, of which 17 were waited for; matrix products, arithmetic and copies ran while one was open for 19% of the time, Pallas kernels for 0%

commit v1 on v0

v1 whole, which is shorter than its diff:
```python
import math

import numpy as np
import jax
import jax.numpy as jnp
from jax import lax
from jax.experimental import pallas as pl
from jax.experimental.pallas import tpu as pltpu
from jax.sharding import PartitionSpec as P

f32 = jnp.float32
bf16 = jnp.bfloat16
D = 512
HEADS = 16
FF = 2048
TOK = 49
SLOT = 64
WINS = 8
RI = 208
R = 416
EPS = 1e-5
SCALE = 32 ** -0.5


def mm(a, b):
    return jnp.dot(a, b, preferred_element_type=f32)


def mm_t(a, b):
    return lax.dot_general(a, b, (((1,), (1,)), ((), ())), preferred_element_type=f32)


def t_mm(a, b):
    return lax.dot_general(a, b, (((0,), (0,)), ((), ())), preferred_element_type=f32)


def permutations():
    out = np.zeros((2, 4 * SLOT, RI), np.float32)
    for w in range(4):
        for t in range(TOK):
            out[0, w * SLOT + t, w * TOK + t] = 1.0
            i = ((w // 2) * 7 + t // 7 + 3) % 14
            j = ((w % 2) * 7 + t % 7 + 3) % 14
            ws, ts = (i // 7) * 2 + j // 7, (i % 7) * 7 + j % 7
            out[1, w * SLOT + t, ws * TOK + ts] = 1.0
    return out


def head_mask():
    return lax.broadcasted_iota(jnp.int32, (SLOT, 128), 1) // 32


def spread(block):
    lane = head_mask()
    zero = jnp.zeros_like(block)
    return jnp.concatenate([jnp.where(lane == h, block, zero) for h in range(4)], axis=0)


def gather_heads(full):
    lane = head_mask()
    out = jnp.zeros((SLOT, 128), f32)
    for h in range(4):
        out = jnp.where(lane == h, full[SLOT * h:SLOT * (h + 1)], out)
    return out


def build_bias(k):
    tabs, idx_ref, bn, bias = k.tabs, k.idx, k.bn, k.bias
    parts = []
    for s in range(2):
        tab = tabs[s]
        hi = tab.astype(bf16)
        rest = tab - hi.astype(f32)
        mid = rest.astype(bf16)
        low = (rest - mid.astype(f32)).astype(bf16)
        parts += [hi, mid, low]
    lhs = jnp.concatenate(parts, axis=0)
    rows_t = lax.broadcasted_iota(jnp.int32, (256, 128), 0)

    def one(i, carry):
        pick = (rows_t == idx_ref[pl.ds(i, 1), :]).astype(f32).astype(bf16)
        got = mm(lhs, pick)
        for s in range(2):
            p = got[48 * s:48 * (s + 1)]
            bn[s, pl.ds(i, 16, stride=SLOT), :] = p[:16] + p[16:32] + p[32:48]
        return carry

    for s in range(2):
        for h in range(HEADS):
            bn[s, SLOT * h + 48:SLOT * (h + 1), :] = jnp.zeros((16, 128), f32)
    lax.fori_loop(0, TOK, one, 0)
    dead = lax.broadcasted_iota(jnp.int32, (SLOT, 256), 0) >= TOK
    for s in range(2):
        for g in range(4):
            turned = jnp.transpose(bn[s, 256 * g:256 * (g + 1), :])[:SLOT]
            bias[s, :, 256 * g:256 * (g + 1)] = jnp.where(dead, -1e30, turned)


def row_loop(step, body):
    def one(i, carry):
        body(pl.ds(pl.multiple_of(i * step, step), step))
        return carry
    lax.fori_loop(0, R // step, one, 0)


def norm_rows(v, gain, offset):
    mean = jnp.mean(v, axis=-1, keepdims=True)
    cen = v - mean
    var = jnp.mean(cen * cen, axis=-1, keepdims=True)
    inv = lax.rsqrt(var + EPS)
    unit = cen * inv
    return unit * gain + offset, unit, inv


def attend_front(k, s):
    sm = k.small

    def ln(rows):
        y, unit, inv = norm_rows(k.u[rows], sm[s, 0:1, :], sm[s, 2:3, :])
        k.tmp[rows] = y.astype(bf16)
        k.n1[s, rows] = unit
        k.inv1[s, rows] = jnp.broadcast_to(inv, (32, 128))
    row_loop(32, ln)
    for m in range(2):
        k.rolled[s, 256 * m:256 * (m + 1), :] = mm(
            k.perm[s], k.tmp[RI * m:RI * (m + 1), :]).astype(bf16)


def project(k, s):
    def one(n, carry):
        cols = pl.ds(pl.multiple_of(n * 256, 256), 256)
        p = mm(k.rolled[s], k.wa[s, :, cols])
        half = pl.ds(pl.multiple_of((n % 2) * 256, 256), 256)
        add_q = jnp.where(n < 2, k.small[s, 4:5, half], 0.0)
        add_v = jnp.where(n >= 4, k.small[s, 5:6, half], 0.0)
        factor = jnp.where(n < 2, SCALE, 1.0)
        k.qkv[s, :, cols] = ((p + (add_q + add_v)) * factor).astype(bf16)
        return carry
    lax.fori_loop(0, 6, one, 0)


def attention(k, s):
    def one(w, carry):
        rows = pl.ds(pl.multiple_of(w * SLOT, SLOT), SLOT)
        for g in range(4):
            lanes = slice(128 * g, 128 * (g + 1))
            q = k.qkv[s, rows, 128 * g:128 * (g + 1)]
            key = k.qkv[s, rows, D + 128 * g:D + 128 * (g + 1)]
            val = k.qkv[s, rows, 2 * D + 128 * g:2 * D + 128 * (g + 1)]
            st = mm_t(key, spread(q)) + k.bias[s, :, 256 * g:256 * (g + 1)]
            if s == 1:
                mk = k.mask[w % 4]
                st = st + jnp.concatenate([mk, mk], axis=1)
            top = jnp.max(st, axis=0, keepdims=True)
            e = jnp.exp(st - top)
            p = e * (1.0 / jnp.sum(e, axis=0, keepdims=True))
            k.probs[s, w, :, 256 * g:256 * (g + 1)] = p
            k.att[rows, lanes] = gather_heads(t_mm(p.astype(bf16), val)).astype(bf16)
        return carry
    lax.fori_loop(0, WINS, one, 0)


def merge_rows(k, s):
    for m in range(2):
        k.unr[s, RI * m:RI * (m + 1), :] = t_mm(
            k.perm[s], k.att[256 * m:256 * (m + 1), :]).astype(bf16)
    sm = k.small

    def one(i, carry):
        rows = pl.ds(pl.multiple_of(i * RI, RI), RI)
        k.mid[rows] = mm(k.unr[s, rows, :], k.wa[s, :, 1536:2048])
        return carry
    lax.fori_loop(0, 2, one, 0)

    def ln(rows):
        middle = k.u[rows] + k.mid[rows] + sm[s, 6:7, :]
        y, unit, inv = norm_rows(middle, sm[s, 1:2, :], sm[s, 3:4, :])
        k.nrm2[s, rows] = y.astype(bf16)
        k.n2[s, rows] = unit
        k.inv2[s, rows] = jnp.broadcast_to(inv, (32, 128))
        k.acc[rows] = middle + sm[s, 7:8, :]
    row_loop(32, ln)


def expand(k, s):
    def one(n, carry):
        cols = pl.ds(pl.multiple_of(n * 256, 256), 256)
        wide = pl.ds(pl.multiple_of(2048 + n * 256, 256), 256)
        pre = mm(k.nrm2[s], k.wa[s, :, wide])
        hb = k.hbias[s, :, cols]
        x = pre + hb
        cdf = 0.5 * (1.0 + lax.erf(x * (1.0 / math.sqrt(2.0))))
        pdf = jnp.exp(-0.5 * x * x) * (1.0 / math.sqrt(2.0 * math.pi))
        k.hid[s, :, cols] = (x * cdf).astype(bf16)
        k.slope[s, :, cols] = (cdf + x * pdf).astype(k.slope.dtype)
        return carry
    lax.fori_loop(0, FF // 256, one, 0)


def reduce_rows(k, s):
    def one(n, carry):
        cols = pl.ds(pl.multiple_of(n * 256, 256), 256)
        k.acc[:, cols] = k.acc[:, cols] + mm(k.hid[s], k.wr[s, :, cols])
        return carry
    lax.fori_loop(0, 2, one, 0)
    for m in range(2):
        half = k.acc[RI * m:RI * (m + 1), :].astype(bf16)
        k.u[RI * m:RI * (m + 1), :] = half.astype(f32)
        k.send_out(s, m, mm(k.perm[0], half).astype(bf16))


def back_ff(k, s):
    def one(n, carry):
        cols = pl.ds(pl.multiple_of(n * 256, 256), 256)
        d = mm_t(k.cot[...], k.wr[s, cols, :]) * k.slope[s, :, cols].astype(f32)
        db = d.astype(bf16)
        k.wr[s, cols, :] = t_mm(k.hid[s, :, cols], k.cot[...]).astype(bf16)
        k.hid[s, :, cols] = db
        k.hgrad[:, cols] = jnp.sum(db.astype(f32), axis=0, keepdims=True)
        return carry
    lax.fori_loop(0, FF // 256, one, 0)
    for q in range(4):
        k.pk[s, 8 + q:9 + q, :] = k.hgrad[:, D * q:D * (q + 1)]
    k.ready(s, "red")

    def three(n, carry):
        rows = pl.ds(pl.multiple_of(n * 256, 256), 256)
        k.dn[:, rows] = mm_t(k.hid[s], k.wa[s, rows, 2048:4096])
        return carry
    lax.fori_loop(0, 2, three, 0)

    def two(n, carry):
        rows = pl.ds(pl.multiple_of(n * 128, 128), 128)
        k.wa[s, rows, 2048:4096] = t_mm(k.nrm2[s, :, rows], k.hid[s]).astype(bf16)
        return carry
    lax.fori_loop(0, 4, two, 0)
    k.ready(s, "exp")


def norm_back_rows(d, unit, inv, gain):
    dg = d * gain
    one = jnp.mean(dg, axis=-1, keepdims=True)
    two = jnp.mean(dg * unit, axis=-1, keepdims=True)
    return inv * (dg - one - unit * two)


def fold8(v):
    return (v[0:8] + v[8:16]) + (v[16:24] + v[24:32])


def back_mid(k, s):
    sm = k.small
    k.sums[...] = jnp.zeros_like(k.sums)

    def nb(rows):
        d = k.dn[rows]
        unit = k.n2[s, rows]
        c = k.cot[rows].astype(f32)
        dm = c + norm_back_rows(d, unit, k.inv2[s, rows, 0:1], sm[s, 1:2, :])
        k.dmid[rows] = dm
        k.tmp[rows] = dm.astype(bf16)
        k.sums[0] += fold8(d * unit)
        k.sums[1] += fold8(d)
        k.sums[2] += fold8(dm)
        k.sums[3] += fold8(c)
    row_loop(32, nb)
    for q, row in ((0, 1), (1, 3), (2, 6), (3, 7)):
        k.pk[s, row:row + 1, :] = jnp.sum(k.sums[q], axis=0, keepdims=True)

    for m in range(2):
        du = mm_t(k.tmp[RI * m:RI * (m + 1), :], k.wa[s, :, 1536:2048]).astype(bf16)
        k.att[256 * m:256 * (m + 1), :] = mm(k.perm[s], du).astype(bf16)

    def one(n, carry):
        rows = pl.ds(pl.multiple_of(n * 256, 256), 256)
        k.wa[s, rows, 1536:2048] = t_mm(k.unr[s, :, rows], k.tmp[...]).astype(bf16)
        return carry
    lax.fori_loop(0, 2, one, 0)
    k.ready(s, "mrg")


def back_attention(k, s):
    k.dbias[...] = jnp.zeros((SLOT, 1024), f32)
    k.qvsum[...] = jnp.zeros_like(k.qvsum)

    def one(w, carry):
        rows = pl.ds(pl.multiple_of(w * SLOT, SLOT), SLOT)
        for g in range(4):
            lanes = slice(128 * g, 128 * (g + 1))
            wide = slice(256 * g, 256 * (g + 1))
            q = k.qkv[s, rows, 128 * g:128 * (g + 1)]
            key = k.qkv[s, rows, D + 128 * g:D + 128 * (g + 1)]
            val = k.qkv[s, rows, 2 * D + 128 * g:2 * D + 128 * (g + 1)]
            da = spread(k.att[rows, lanes])
            p = k.probs[s, w, :, wide]
            dp = mm_t(val, da)
            ds = p * (dp - jnp.sum(p * dp, axis=0, keepdims=True))
            k.dbias[:, wide] += ds
            dsb = ds.astype(bf16)
            dv = mm(p.astype(bf16), da)
            dk = mm(dsb, spread(q))
            dq = gather_heads(t_mm(dsb, key)) * SCALE
            k.qkv[s, rows, 128 * g:128 * (g + 1)] = dq.astype(bf16)
            k.qkv[s, rows, D + 128 * g:D + 128 * (g + 1)] = dk.astype(bf16)
            k.qkv[s, rows, 2 * D + 128 * g:2 * D + 128 * (g + 1)] = dv.astype(bf16)
            k.qvsum[0, :, lanes] += fold8(dq[:32]) + fold8(dq[32:])
            k.qvsum[1, :, lanes] += fold8(dv[:32]) + fold8(dv[32:])
        return carry
    lax.fori_loop(0, WINS, one, 0)
    for q in range(2):
        k.pk[s, 4 + q:5 + q, :] = jnp.sum(k.qvsum[q], axis=0, keepdims=True)


def back_att_grads(k, s):
    def one(n, carry):
        rows = pl.ds(pl.multiple_of(n * 128, 128), 128)
        k.ga[s, rows, :] = t_mm(k.rolled[s, :, rows], k.qkv[s]).astype(bf16)
        return carry
    lax.fori_loop(0, 4, one, 0)
    k.ready(s, "att")


def back_input(k, s):
    sm = k.small

    def one(n, carry):
        rows = pl.ds(pl.multiple_of(n * 256, 256), 256)
        k.att[:, rows] = mm_t(k.qkv[s], k.wa[s, rows, 0:1536]).astype(bf16)
        return carry
    lax.fori_loop(0, 2, one, 0)
    for m in range(2):
        k.dn[RI * m:RI * (m + 1), :] = t_mm(k.perm[s], k.att[256 * m:256 * (m + 1), :])
    k.sums[...] = jnp.zeros_like(k.sums)

    def nb(rows):
        d = k.dn[rows].astype(bf16).astype(f32)
        unit = k.n1[s, rows]
        di = k.dmid[rows] + norm_back_rows(d, unit, k.inv1[s, rows, 0:1], sm[s, 0:1, :])
        k.cot[rows] = di.astype(bf16)
        k.sums[0] += fold8(d * unit)
        k.sums[1] += fold8(d)
    row_loop(32, nb)
    for q, row in ((0, 0), (1, 2)):
        k.pk[s, row:row + 1, :] = jnp.sum(k.sums[q], axis=0, keepdims=True)
    for m in range(2):
        k.send_grad(s, m, mm(k.perm[0], k.cot[RI * m:RI * (m + 1), :]).astype(bf16))


def table_grad(k, s):
    bn = k.bn
    for g in range(4):
        bn[0, 256 * g:256 * (g + 1), 0:SLOT] = jnp.transpose(k.dbias[:, 256 * g:256 * (g + 1)])
    rows_t = lax.broadcasted_iota(jnp.int32, (256, 128), 0)
    lane = lax.broadcasted_iota(jnp.int32, (16, 128), 1)

    def one(i, acc):
        pick = (rows_t == k.idx[pl.ds(i, 1), :]).astype(f32).astype(bf16)
        x = jnp.where(lane < TOK, bn[0, pl.ds(i, 16, stride=SLOT), :], 0.0)
        hi = x.astype(bf16)
        low = (x - hi.astype(f32)).astype(bf16)
        got = mm_t(jnp.concatenate([hi, low], axis=0), pick)
        return acc + got[:16] + got[16:]
    total = lax.fori_loop(0, TOK, one, jnp.zeros((16, 256), f32))
    k.pk[s, 12:20, 0:256] = total[:8]
    k.pk[s, 12:20, 256:512] = total[8:]


def load_input(k, src, dst_f32=None, dst_b16=None):
    tok = lax.broadcasted_iota(jnp.int32, (256, D), 0) % SLOT
    for m in range(2):
        x = src[m].reshape(256, D)
        x = jnp.where(tok < TOK, x, jnp.zeros_like(x))
        c = t_mm(k.perm[0], x)
        if dst_f32 is not None:
            dst_f32[RI * m:RI * (m + 1), :] = c
        if dst_b16 is not None:
            dst_b16[RI * m:RI * (m + 1), :] = c.astype(bf16)


MESH = pl.DeviceIdType.MESH
PIECES = (
    ("s", 0, 128), ("a", 0, 512), ("a", 512, 1024), ("a", 1024, 1536), ("a", 1536, 2048),
    ("a", 2048, 3072), ("a", 3072, 4096), ("r", 0, 256), ("r", 256, 512),
)
SHARD = {"s": 16, "a": 32, "r": 128}
FINISHED = {
    "red": (("r", 0, 256), ("r", 256, 512)),
    "exp": (("a", 2048, 3072), ("a", 3072, 4096)),
    "mrg": (("a", 1536, 2048),),
    "att": (("a", 0, 512), ("a", 512, 1024), ("a", 1024, 1536)),
}
PER_BLOCK = 8


def scratch():
    V = pltpu.VMEM
    S = pltpu.SemaphoreType.DMA
    return dict(
        wa=V((2, 512, 4096), bf16), wr=V((2, 2048, 512), bf16), ws=V((2, 256, 128), bf16),
        ga=V((2, 512, 1536), bf16),
        xin=V((2, 4, SLOT, D), bf16), cin=V((2, 4, SLOT, D), bf16), mask=V((4, SLOT, 128), bf16),
        tabs=V((2, 16, 256), f32), small=V((2, 8, D), f32), hbias=V((2, 1, FF), f32),
        u=V((R, D), f32), tmp=V((R, D), bf16), acc=V((R, D), f32), dn=V((R, D), f32),
        n1=V((2, R, D), f32), inv1=V((2, R, 128), f32), n2=V((2, R, D), f32), inv2=V((2, R, 128), f32),
        rolled=V((2, 512, D), bf16), qkv=V((2, 512, 3 * D), bf16), probs=V((2, WINS, SLOT, 1024), f32),
        att=V((512, D), bf16), unr=V((2, R, D), bf16), nrm2=V((2, R, D), bf16),
        hid=V((2, R, FF), bf16), slope=V((2, R, FF), bf16), cot=V((R, D), bf16),
        sums=V((4, 8, D), f32), qvsum=V((2, 8, D), f32), hgrad=V((1, FF), f32),
        bias=V((2, SLOT, 1024), f32), bn=V((2, 1024, 128), f32), dbias=V((SLOT, 1024), f32),
        pk=V((2, 24, D), f32), pk_c=V((2, 24, D), f32), pk_y=V((2, 24, D), f32), pk_z=V((4, 24, D), f32),
        got_c=V((2, 24, D), f32), got_y=V((2, 24, D), f32), got_x=V((24, D), f32),
        ca=V((2, 256, 4096), bf16), cr=V((2, 1024, 512), bf16),
        ya=V((2, 64, 4096), bf16), yr=V((2, 256, 512), bf16),
        yba=V((64, 4096), bf16), ybr=V((256, 512), bf16),
        xba=V((2, 64, 4096), bf16), xbr=V((2, 256, 512), bf16),
        xaa=V((64, 4096), bf16), xar=V((256, 512), bf16),
        za=V((3, 32, 4096), bf16), zr=V((3, 128, 512), bf16),
        g_send=S((len(PIECES), 11)), g_recv=S((len(PIECES), 11)), g_own=S((len(PIECES),)),
        r_send=S((2 * PER_BLOCK, 10)), r_recv=S((2 * PER_BLOCK, 10)),
        p_send=S((2, 6)), p_recv=S((2, 6)),
        i_send=S((3, 3)), i_recv=S((3, 3)), i_own=S((3,)),
        t_send=S((1,)), t_recv=S((1,)), t_own=S((1,)),
        o_send=S((2, 2, 4)), o_recv=S((2, 8)),
    )


ALIASES = {"mid": "dn", "dmid": "u"}


class Kernel:
    def __init__(self, refs, sub):
        self.__dict__.update(refs)
        for name, other in ALIASES.items():
            setattr(self, name, getattr(self, other))
        self.px = lax.axis_index("pipe")
        self.w = lax.axis_index("win")
        self.z = lax.axis_index("fsdp")
        self.y, self.c = self.w // 2, self.w % 2
        self.g, self.low = self.z // sub, self.z % sub
        self.sub = sub
        self.wy = (1 - self.y) * 2 + self.c
        self.wc = self.y * 2 + 1 - self.c
        self.wyc = (1 - self.y) * 2 + 1 - self.c
        self.own, self.other = self.px, 1 - self.px
        self.at_x = self.device(1 - self.px, self.w, self.z)
        self.at_y = self.device(self.px, self.wy, self.z)
        self.at_c = self.device(self.px, self.wc, self.z)
        self.flying = []
        self.pending = []
        self.reduced = 0

    def device(self, pipe, win, fsdp):
        return {"pipe": pipe, "win": win, "fsdp": fsdp}

    def at_z(self, d):
        return self.device(self.px, self.w, ((self.g + d) % 4) * self.sub + self.low)

    def barrier(self):
        sem = pltpu.get_barrier_semaphore()
        peers = [self.at_z(d) for d in (1, 2, 3)]
        for dw in range(4):
            for dp in range(2):
                if dw or dp:
                    peers.append(self.device((self.px + dp) % 2, (self.w + dw) % 4, self.z))
        for peer in peers:
            pl.semaphore_signal(sem, inc=1, device_id=peer, device_id_type=MESH)
        pl.semaphore_wait(sem, len(peers))

    def move(self, src, dst, send, recv, device):
        return pltpu.make_async_remote_copy(
            src_ref=src, dst_ref=dst, send_sem=send, recv_sem=recv, device_id=device, device_id_type=MESH)

    def inputs(self, start):
        for which, (src, dst) in enumerate(((self.x_h, self.xin), (self.c_h, self.cin), (self.m_h, self.mask))):
            def part(v):
                return src if which == 2 else src.at[pl.ds(8 * self.px + 2 * v, 2)]

            def place(v):
                return dst.at[v] if which == 2 else dst.at[:, v]
            if start:
                pltpu.make_async_copy(part(self.w), place(self.w), self.i_own.at[which]).start()
                for d in (1, 2, 3):
                    v = (self.w + d) % 4
                    self.move(part(v), place(self.w), self.i_send.at[which, d - 1], self.i_recv.at[which, d - 1],
                              self.device(self.px, v, self.z)).start()

    def input_done(self, which):
        src, dst = ((self.x_h, self.xin), (self.c_h, self.cin), (self.m_h, self.mask))[which]
        mine = src if which == 2 else src.at[pl.ds(8 * self.px + 2 * self.w, 2)]

        def place(v):
            return dst.at[v] if which == 2 else dst.at[:, v]
        pltpu.make_async_copy(mine, place(self.w), self.i_own.at[which]).wait()
        for d in (1, 2, 3):
            copy = self.move(mine, place((self.w + 4 - d) % 4), self.i_send.at[which, d - 1],
                             self.i_recv.at[which, d - 1], self.at_x)
            copy.wait_recv()
            copy.wait_send()

    def tables(self, start):
        own = pltpu.make_async_copy(self.tab_h, self.tabs.at[self.px], self.t_own.at[0])
        if start:
            own.start()
            self.move(self.tab_h, self.tabs.at[self.px], self.t_send.at[0], self.t_recv.at[0], self.at_x).start()
        else:
            own.wait()
            copy = self.move(self.tab_h, self.tabs.at[self.other], self.t_send.at[0], self.t_recv.at[0], self.at_x)
            copy.wait_recv()
            copy.wait_send()

    def spot(self, e, block, row, rows):
        kind, lo, hi = PIECES[e]
        ref = {"s": self.ws, "a": self.wa, "r": self.wr}[kind]
        rows_at = pl.ds(pl.multiple_of(row, 16), rows)
        return ref.at[block, rows_at, pl.ds(lo, hi - lo)]

    def line(self, e, block, win, half=None):
        rows = SHARD[PIECES[e][0]] * 4
        if half is None:
            return self.spot(e, block, win * rows, rows)
        return self.spot(e, block, win * rows + half * (rows // 2), rows // 2)

    def shard_src(self, e):
        kind, lo, hi = PIECES[e]
        if kind == "s":
            return self.sp_h
        if kind == "r":
            return self.red_h.at[:, pl.ds(lo, hi - lo)]
        for ref, at in ((self.att_h, 0), (self.mrg_h, 1536), (self.exp_h, 2048)):
            if at <= lo < at + ref.shape[1]:
                return ref.at[:, pl.ds(lo - at, hi - lo)]

    def shard_spot(self, e, g):
        rows = SHARD[PIECES[e][0]]
        return self.spot(e, self.own, (self.w * 4 + g) * rows, rows)

    def send(self, e, n, src, device):
        self.move(src, src, self.g_send.at[e, n], self.g_recv.at[e, n], device).start()

    def landed(self, e, n, place):
        self.move(place, place, self.g_send.at[e, 0], self.g_recv.at[e, n], self.at_x).wait_recv()

    def gather_start(self, e):
        src = self.shard_src(e)
        pltpu.make_async_copy(src, self.shard_spot(e, self.g), self.g_own.at[e]).start()
        for d in (1, 2, 3):
            self.move(src, self.shard_spot(e, self.g), self.g_send.at[e, d - 1], self.g_recv.at[e, d - 1],
                      self.at_z(d)).start()

    def gather_one(self, e):
        pltpu.make_async_copy(self.shard_src(e), self.shard_spot(e, self.g), self.g_own.at[e]).wait()
        for d in (1, 2, 3):
            self.landed(e, d - 1, self.shard_spot(e, (self.g + 4 - d) % 4))
        mine = self.line(e, self.own, self.w)
        self.send(e, 3, mine, self.at_x)
        self.send(e, 4, mine, self.at_y)
        self.send(e, 5, mine, self.at_c)

    def gather_two(self, e):
        got = self.line(e, self.other, self.w)
        self.landed(e, 3, got)
        self.send(e, 6, self.line(e, self.other, self.w, 0), self.at_y)
        self.send(e, 7, got, self.at_c)
        got = self.line(e, self.own, self.wy)
        self.landed(e, 4, got)
        self.send(e, 8, self.line(e, self.own, self.wy, 1), self.at_x)
        self.send(e, 9, got, self.at_c)

    def gather_three(self, e):
        self.landed(e, 6, self.line(e, self.other, self.wy, 0))
        self.landed(e, 8, self.line(e, self.other, self.wy, 1))
        self.send(e, 10, self.line(e, self.other, self.wy), self.at_c)

    def gathered(self, e, block):
        mine = self.px == block
        self.landed(e, jnp.where(mine, 5, 7), self.line(e, block, self.wc))
        self.landed(e, jnp.where(mine, 9, 10), self.line(e, block, self.wyc))

    def tick(self, i):
        n = len(PIECES)
        if i < n:
            self.gather_one(i)
        if 0 <= i - 1 < n:
            self.gather_two(i - 1)
        if 0 <= i - 2 < n:
            self.gather_three(i - 2)

    def gather_sent(self, e):
        mine = self.line(e, self.own, self.w)
        half = self.line(e, self.own, self.w, 0)
        shard = self.shard_spot(e, self.g)
        for n in range(11):
            src = shard if n < 3 else half if n in (6, 8) else mine
            self.move(src, src, self.g_send.at[e, n], self.g_recv.at[e, n], self.at_x).wait_send()

    def decode(self):
        for s in range(2):
            for win in range(4):
                total = jnp.zeros((8, 128), f32)
                for g in range(4):
                    r = win * 4 + g
                    total = total + self.ws[s, 16 * r:16 * r + 16, :].astype(f32)[:8]
                    self.hbias[s, :, 128 * r:128 * (r + 1)] = self.ws[s, 16 * r:16 * r + 16, :].astype(f32)[8:9]
                self.small[s, :, 128 * win:128 * (win + 1)] = total

    def send_out(self, s, m, value):
        self.emit(0, s, m, value)

    def send_grad(self, s, m, value):
        self.emit(1, s, m, value)

    def emit(self, which, s, m, value):
        stage = (self.xin, self.cin)[s]
        dst = (self.out_h, self.grad_h)[which]
        if m == 0 and which == 1:
            self.emitted(0, s)
        for v in range(4):
            stage[m, v] = value[SLOT * v:SLOT * (v + 1)]
        if m == 0:
            return
        at = pl.ds(8 * self.px + 2 * self.w, 2)
        for v in range(4):
            here = (self.px == s) & (self.w == v)
            recv = self.o_recv.at[which, self.px * 4 + self.w]

            @pl.when(here)
            def _():
                pltpu.make_async_copy(stage.at[:, v], dst.at[at], recv).start()

            @pl.when(jnp.logical_not(here))
            def _():
                self.move(stage.at[:, v], dst.at[at], self.o_send.at[which, s, v], recv,
                          self.device(s, v, self.z)).start()

    def emitted(self, which, s):
        stage = (self.xin, self.cin)[s]
        dst = (self.out_h, self.grad_h)[which]
        at = pl.ds(8 * self.px + 2 * self.w, 2)
        for v in range(4):
            here = (self.px == s) & (self.w == v)
            recv = self.o_recv.at[which, self.px * 4 + self.w]

            @pl.when(here)
            def _():
                pltpu.make_async_copy(stage.at[:, v], dst.at[at], recv).wait()

            @pl.when(jnp.logical_not(here))
            def _():
                self.move(stage.at[:, v], dst.at[at], self.o_send.at[which, s, v], recv,
                          self.device(s, v, self.z)).wait_send()

    def arrived(self, which):
        dst = (self.out_h, self.grad_h)[which]
        for p in range(2):
            for v in range(4):
                from_here = (self.px == p) & (self.w == v)

                @pl.when(jnp.logical_not(from_here))
                def _():
                    place = dst.at[pl.ds(8 * p + 2 * v, 2)]
                    self.move(place, place, self.o_send.at[which, 0, 0], self.o_recv.at[which, p * 4 + v],
                              self.at_x).wait_recv()

    def ready(self, s, kind):
        fresh = []
        for piece in FINISHED[kind]:
            fresh.append([s, piece, self.reduced, 0])
            self.reduced += 1
        self.pump()
        for job in fresh:
            self.advance(job)
        self.flying += fresh

    def pump(self):
        for job in self.flying:
            self.advance(job)
        self.flying = [job for job in self.flying if job[3] < 5]

    def advance(self, job):
        (self.reduce_zero, self.reduce_one, self.reduce_two, self.reduce_three, self.reduce_four)[job[3]](*job[:3])
        job[3] += 1

    def part(self, piece):
        kind, lo, hi = piece
        grads = self.wr if kind == "r" else self.ga if hi <= 1536 else self.wa
        bufs = (self.cr, self.yr, self.ybr, self.xbr, self.xar, self.zr) if kind == "r" else (
            self.ca, self.ya, self.yba, self.xba, self.xaa, self.za)
        return grads, bufs, SHARD[kind], pl.ds(lo, hi - lo)

    def add(self, grads, s, row, src, rows, cols):
        step = 16 if cols.size > 512 else 32

        def one(i, carry):
            at = pl.ds(pl.multiple_of(row + i * step, 16), step)
            here = pl.ds(pl.multiple_of(i * step, 16), step)
            grads[s, at, cols] = (grads[s, at, cols].astype(f32) + src[here, cols].astype(f32)).astype(bf16)
            return carry
        lax.fori_loop(0, rows // step, one, 0)

    def cut(self, grads, s, row, rows, cols):
        return grads.at[s, pl.ds(pl.multiple_of(row, 16), rows), cols]

    def throw(self, q, n, src, dst, device):
        self.move(src, dst, self.r_send.at[q, n], self.r_recv.at[q, n], device).start()

    def caught(self, q, n, place):
        self.move(place, place, self.r_send.at[q, n], self.r_recv.at[q, n], self.at_x).wait_recv()

    def thrown(self, q, n, src):
        self.move(src, src, self.r_send.at[q, n], self.r_recv.at[q, n], self.at_x).wait_send()

    def reduce_zero(self, s, piece, q):
        grads, bufs, rps, cols = self.part(piece)
        lr = 4 * rps
        for v in range(2):
            src = self.cut(grads, s, (2 * v + 1 - self.c) * lr, lr, cols)
            self.throw(q, v, src, bufs[0].at[s, pl.ds(v * lr, lr), cols], self.at_c)

    def reduce_one(self, s, piece, q):
        grads, bufs, rps, cols = self.part(piece)
        lr, half = 4 * rps, 2 * rps
        for v in range(2):
            place = bufs[0].at[s, pl.ds(v * lr, lr), cols]
            self.caught(q, v, place)
            self.add(grads, s, (2 * v + self.c) * lr, bufs[0].at[s, pl.ds(v * lr, lr)], lr, cols)
        self.throw(q, 2, self.cut(grads, s, self.wy * lr, half, cols), bufs[1].at[s, :, cols], self.at_y)

        @pl.when(self.px != s)
        def _():
            self.throw(q, 3, self.cut(grads, s, self.w * lr + half, half, cols), bufs[3].at[0, :, cols], self.at_x)
            self.throw(q, 4, self.cut(grads, s, self.wy * lr + half, half, cols), bufs[3].at[1, :, cols], self.at_x)

    def reduce_two(self, s, piece, q):
        grads, bufs, rps, cols = self.part(piece)
        lr, half = 4 * rps, 2 * rps
        self.caught(q, 2, bufs[1].at[s, :, cols])
        self.add(grads, s, self.w * lr, bufs[1].at[s], half, cols)

        @pl.when(self.px != s)
        def _():
            self.throw(q, 5, self.cut(grads, s, self.w * lr, half, cols), bufs[4].at[:, cols], self.at_x)

        @pl.when(self.px == s)
        def _():
            for n, win in ((0, self.w), (1, self.wy)):
                self.caught(q, 3 + n, bufs[3].at[n, :, cols])
                self.add(grads, s, win * lr + half, bufs[3].at[n], half, cols)
            self.throw(q, 6, self.cut(grads, s, self.wy * lr + half, half, cols), bufs[2].at[:, cols], self.at_y)

    def reduce_three(self, s, piece, q):
        grads, bufs, rps, cols = self.part(piece)
        lr, half = 4 * rps, 2 * rps

        @pl.when(self.px == s)
        def _():
            self.caught(q, 5, bufs[4].at[:, cols])
            self.add(grads, s, self.w * lr, bufs[4], half, cols)
            self.caught(q, 6, bufs[2].at[:, cols])
            self.add(grads, s, self.w * lr + half, bufs[2], half, cols)
            for d in (1, 2, 3):
                row = (self.w * 4 + (self.g + d) % 4) * rps
                self.throw(q, 6 + d, self.cut(grads, s, row, rps, cols), bufs[5].at[d - 1, :, cols], self.at_z(d))

    def reduce_four(self, s, piece, q):
        grads, bufs, rps, cols = self.part(piece)
        lr, half = 4 * rps, 2 * rps
        kind, lo, hi = piece
        out, at = self.o_red, 0
        if kind == "a":
            out, at = ((self.o_att, 0), (self.o_mrg, 1536), (self.o_exp, 2048))[
                0 if lo < 1536 else 1 if lo < 2048 else 2]
        to = pl.ds(lo - at, hi - lo)

        @pl.when(self.px == s)
        def _():
            for d in (1, 2, 3):
                self.caught(q, 6 + d, bufs[5].at[d - 1, :, cols])
            base = (self.w * 4 + self.g) * rps

            def one(i, carry):
                rows = pl.ds(pl.multiple_of(i * 16, 16), 16)
                total = grads[s, pl.ds(pl.multiple_of(base + i * 16, 16), 16), cols].astype(f32)
                for n in range(3):
                    total = total + bufs[5][n, rows, cols].astype(f32)
                out[rows, to] = total
                return carry
            lax.fori_loop(0, rps // 16, one, 0)

        for n in (0, 1):
            self.thrown(q, n, self.cut(grads, s, 0, lr, cols))
        self.thrown(q, 2, self.cut(grads, s, 0, half, cols))

        @pl.when(self.px != s)
        def _():
            for n in (3, 4, 5):
                self.thrown(q, n, self.cut(grads, s, 0, half, cols))

        @pl.when(self.px == s)
        def _():
            self.thrown(q, 6, self.cut(grads, s, 0, half, cols))
            for n in (7, 8, 9):
                self.thrown(q, n, self.cut(grads, s, 0, rps, cols))

    def small_step(self, s, step):
        def copy(n, src, dst, device):
            return self.move(src, dst, self.p_send.at[s, n], self.p_recv.at[s, n], device)
        first = copy(0, self.pk.at[s], self.got_c.at[s], self.at_c)
        second = copy(1, self.pk_c.at[s], self.got_y.at[s], self.at_y)
        third = copy(2, self.pk_y.at[s], self.got_x, self.at_x)
        last = [copy(2 + d, self.pk_z.at[self.g], self.pk_z.at[self.g], self.at_z(d)) for d in (1, 2, 3)]
        if step == 0:
            first.start()
        if step == 1:
            first.wait_recv()
            self.pk_c[s] = self.pk[s] + self.got_c[s]
            second.start()
        if step == 2:
            second.wait_recv()
            self.pk_y[s] = self.pk_c[s] + self.got_y[s]

            @pl.when(self.px != s)
            def _():
                third.start()
        if step == 3:
            @pl.when(self.px == s)
            def _():
                third.wait_recv()
                self.pk_z[self.g] = self.pk_y[s] + self.got_x[...]
                for c in last:
                    c.start()
        if step == 4:
            first.wait_send()
            second.wait_send()

            @pl.when(self.px != s)
            def _():
                third.wait_send()

            @pl.when(self.px == s)
            def _():
                for d in (1, 2, 3):
                    place = self.pk_z.at[(self.g + 4 - d) % 4]
                    copy(2 + d, place, place, self.at_x).wait_recv()
                    last[d - 1].wait_send()
                self.o_pk[...] = ((self.pk_z[0] + self.pk_z[1]) + self.pk_z[2]) + self.pk_z[3]


def program(k):
    k.barrier()
    for e in range(4):
        k.gather_start(e)
        if e == 0:
            k.inputs(True)
            k.tables(True)
    for e in range(4, len(PIECES)):
        k.gather_start(e)
    k.tables(False)
    k.tick(0)
    build_bias(k)
    k.tick(1)
    k.tick(2)
    for which in range(3):
        k.input_done(which)
    for s in range(2):
        k.gathered(0, s)
    k.decode()
    load_input(k, k.xin, dst_f32=k.u)
    load_input(k, k.cin, dst_b16=k.cot)
    for s in range(2):
        attend_front(k, s)
        for e in (1, 2, 3):
            if s == 0:
                k.tick(e + 2)
        for e in (1, 2, 3):
            k.gathered(e, s)
        project(k, s)
        attention(k, s)
        if s == 0:
            k.tick(6)
        k.gathered(4, s)
        merge_rows(k, s)
        if s == 0:
            k.tick(7)
            k.tick(8)
        k.gathered(5, s)
        k.gathered(6, s)
        expand(k, s)
        if s == 0:
            k.tick(9)
            k.tick(10)
        k.gathered(7, s)
        k.gathered(8, s)
        reduce_rows(k, s)
    for e in range(len(PIECES)):
        k.gather_sent(e)
    for s in (1, 0):
        back_ff(k, s)
        back_mid(k, s)
        back_attention(k, s)
        back_att_grads(k, s)
        table_grad(k, s)
        back_input(k, s)
        k.small_step(s, 0)
        if s == 1:
            k.pump()
            for step in range(1, 5):
                k.small_step(s, step)
    step = 1
    while k.flying or step < 5:
        k.pump()
        if step < 5:
            k.small_step(0, step)
        step += 1
    k.arrived(0)
    k.arrived(1)
    k.emitted(1, 1)
    k.emitted(1, 0)


INPUTS = ("x_h", "c_h", "att_h", "mrg_h", "exp_h", "red_h", "sp_h", "tab_h", "m_h", "idx", "perm")
OUTPUTS = ("out_h", "grad_h", "o_att", "o_mrg", "o_exp", "o_red", "o_pk")


def both_blocks(sub, *operands):
    names = scratch()

    def body(*refs):
        all_names = INPUTS + OUTPUTS + tuple(names)
        program(Kernel(dict(zip(all_names, refs)), sub))
    S = jax.ShapeDtypeStruct
    images = operands[0].shape[0]
    anywhere = pl.BlockSpec(memory_space=pl.ANY)
    local = pl.BlockSpec(memory_space=pltpu.VMEM)
    return pl.pallas_call(
        body,
        out_shape=(
            S((images, SLOT, D), bf16), S((images, SLOT, D), bf16), S((32, 1536), f32), S((32, 512), f32),
            S((32, 2048), f32), S((128, 512), f32), S((24, D), f32)),
        in_specs=[anywhere] * 9 + [local] * 2,
        out_specs=[anywhere] * 2 + [local] * 5,
        scratch_shapes=[names[n] for n in names],
        compiler_params=pltpu.CompilerParams(
            collective_id=0, has_side_effects=True, vmem_limit_bytes=67043328),
    )(*operands)


def shards(block_input, out_grad, norm_gains, norm_offsets, attend_weight, row_biases, position_table,
           merge_weight, expand_weight, hidden_biases, reduce_weight, window_mask, position_index):
    fsdp = lax.axis_size("fsdp")
    sub = fsdp // 4
    z = lax.axis_index("fsdp")
    group = z // sub
    groups = [[g * sub + i for i in range(sub)] for g in range(4)]

    def whole(shard, axis):
        if sub == 1:
            return shard
        return lax.all_gather(shard, "fsdp", axis=axis, axis_index_groups=groups, tiled=True)

    att = whole(attend_weight[0], 0)
    mrg = whole(merge_weight[0], 0)
    exp = whole(expand_weight[0], 0)
    red = whole(reduce_weight[0], 0)
    rows = jnp.concatenate([norm_gains[0], norm_offsets[0], row_biases[0]], axis=0)
    rows = whole(rows, 1)
    hid = whole(hidden_biases[0], 0)
    at = jnp.arange(128, dtype=jnp.int32) // 32 == group
    placed = jnp.where(at[None, :], jnp.tile(rows, (1, 4)), jnp.zeros((), bf16))
    small = jnp.concatenate([placed, hid[None, :], jnp.zeros((7, 128), bf16)], axis=0)
    table = jnp.pad(position_table[0].T, ((0, 0), (0, 256 - position_table.shape[1])))
    mask = jnp.pad(jnp.where(window_mask[0].T > 0, -100.0, 0.0).astype(bf16), ((0, SLOT - TOK), (0, SLOT - TOK)))
    mask = jnp.concatenate([mask, mask], axis=1)
    idx = jnp.pad(position_index, ((0, 56 - TOK), (0, 128 - TOK)), constant_values=-1)
    perm = jnp.asarray(permutations(), bf16)
    spread_out = ((0, 0), (0, SLOT - TOK), (0, 0))
    x = jnp.pad(block_input[:, 0], spread_out)
    c = jnp.pad(out_grad[:, 0], spread_out)
    out, grad, g_att, g_mrg, g_exp, g_red, pk = both_blocks(
        sub, x, c, att, mrg, exp, red, small, table, mask, idx, perm)

    def mine(total, axis):
        if sub == 1:
            return total
        return lax.psum_scatter(total, "fsdp", scatter_dimension=axis, axis_index_groups=groups, tiled=True)

    def spread_sum(total):
        if sub == 1:
            return total
        return lax.psum(total, "fsdp", axis_index_groups=groups)

    pk = spread_sum(pk)
    r = lax.axis_index("win") * fsdp + z
    width = D // (4 * fsdp)
    sums = lax.dynamic_slice(pk, (0, r * width), (8, width))
    hidden = lax.dynamic_slice(pk[8:12].reshape(1, FF), (0, r * 4 * width), (1, 4 * width))
    tab = jnp.concatenate([pk[12:20, :256], pk[12:20, 256:]], axis=0)[:, :position_table.shape[1]].T
    return (
        out[:, :TOK].reshape((1,) + block_input.shape),
        grad[:, :TOK].astype(f32).reshape((1,) + block_input.shape),
        sums[None, 0:2], sums[None, 2:4], mine(g_att, 0)[None], sums[None, 4:8], tab[None],
        mine(g_mrg, 0)[None], mine(g_exp, 0)[None], hidden, mine(g_red, 0)[None],
    )


def solution(mesh):
    placed = (
        P("fsdp", "win", None, None),
        P("fsdp", "win", None, None),
        P("pipe", None, ("win", "fsdp")),
        P("pipe", None, ("win", "fsdp")),
        P("pipe", ("win", "fsdp"), None),
        P("pipe", None, ("win", "fsdp")),
        P("pipe", None, None),
        P("pipe", ("win", "fsdp"), None),
        P("pipe", ("win", "fsdp"), None),
        P("pipe", ("win", "fsdp")),
        P("pipe", ("win", "fsdp"), None),
        P("win", None, None),
        P(),
    )
    return jax.shard_map(
        shards,
        mesh=mesh,
        in_specs=placed,
        out_specs=(
            P("pipe", "fsdp", "win", None, None),
            P("pipe", "fsdp", "win", None, None),
            P("pipe", None, ("win", "fsdp")),
            P("pipe", None, ("win", "fsdp")),
            P("pipe", ("win", "fsdp"), None),
            P("pipe", None, ("win", "fsdp")),
            P("pipe", None, None),
            P("pipe", ("win", "fsdp"), None),
            P("pipe", ("win", "fsdp"), None),
            P("pipe", ("win", "fsdp")),
            P("pipe", ("win", "fsdp"), None),
        ),
        check_vma=False,
    )
```

time: 1210 us -> 282 us (0.23)
  waiting for transfers between devices: 417 us -> 0 us
  Pallas kernels: 0 us -> 257 us
  local copies, waits for them, and re-layouts: 262 us -> 18.5 us
  blocking collectives: 235 us -> 0 us
  matrix products: 162 us -> 0 us
  other arithmetic: 92.9 us -> 5.1 us
  between operations: 17.2 us -> 0.72 us
  starting transfers between devices: 12.9 us -> 0 us
    reduce_scatter x4 -> x0, waiting for transfers between devices: 282 us -> none  [the longest x1 76.3 us: shards(): lax.psum_scatter(running[6], ('win', 'fsdp'), scatter_dimension=0, tiled=...]
    pallas_call x0 -> x1, Pallas kernels: none -> 257 us  [both_blocks(): pl.pallas_call(body, out_shape=(S((images, SLOT, D), bf16), S((images, SL...]
    all_gather x5 -> x0, blocking collectives: 171 us -> none  [the longest x1 38.3 us: shards(): lax.all_gather(local_shard[4], ('win', 'fsdp'), axis=0, tiled=True)]
    dot_general x39 -> x0, matrix products: 162 us -> none  [the longest x8 34.3 us: matmul(): return jnp.dot(operand, other, preferred_element_type=jnp.float32)]
    ppermute x18 -> x0, waiting for transfers between devices: 93.2 us -> none  [the longest x16 58.8 us: partner(): return lax.ppermute(block, axis, route)]
    reshape x25 -> x0, local copies, waits for them, and re-layouts: 74.8 us -> none  [the longest x4 19.1 us: roll_ahead(): return window_grid.reshape(windows.shape)]
    psum x1 -> x0, blocking collectives: 64.1 us -> none  [shards(): table_grads = lax.psum(table_local, ('win', 'fsdp'))]
    convert_element_type x20 -> x0, local copies, waits for them, and re-layouts: 63.5 us -> none  [the longest x8 43.7 us: attention_forward(): attended.reshape(grid_shape).astype(jnp.bfloat16)]
  transfers between devices with their start and end apart: 28 -> 0, of which waited for: 17 -> 0; matrix products, arithmetic and copies ran while one was open for 19% -> 0% of each run, Pallas kernels for 0% -> 0%
where the time goes in v1:
time: 282 us; the launch traced here: 281 us
  Pallas kernels  257 us (91%)
  local copies, waits for them, and re-layouts  18.5 us (7%)
  other arithmetic  5.1 us (2%)
    pallas_call x1, Pallas kernels, both_blocks(): pl.pallas_call(body, out_shape=(S((images, SLOT, D), bf16), S((images, SL...  257 us
    unnamed x21, local copies, waits for them, and re-layouts  10.3 us

profile of v1, /device:TPU:0, one launch (start us, length us, event | category | flops | bytes accessed | tf_op | source)
XLA Modules:
  0.0 281.4 jit_solution(17133697201500609685)
XLA Ops:
  0.7 0.1 pad.30.clone
  0.7 0.7 pad_maximum_fusion.2
  1.5 0.1 tile.10
  1.6 1.3 maximum_maximum_fusion.refs_6_
  2.9 1.3 pad.21.refs_7_
  4.2 0.8 copy.27
  5.1 0.7 pad_maximum_fusion.1.refs_8_
  5.8 1.4 pad.23.refs_9_
  7.1 0.0 copy-start
  7.1 1.7 copy.34
  8.8 1.1 pad.19.refs_0_
  9.9 0.0 copy-done
  9.9 0.4 copy.33
  10.3 1.1 pad.20.refs_1_
  11.4 257.1 %shard_map.221 = (bf16[16,64,512]{2,1,0:T(8,128)(2,1)}, bf16[16,64,512]{2,1,0:T(8,128)(2,1)}, f32[32,1536]{1,0:T(8,128)}, f32[32,512]{1,0:T(8,128)}, f32[32,2048...) custom-call(bf16[16,64,512]{2,1,0:T(8,128)(2,1)} %pad.19.refs_0_, bf16[16,64,512]{2,1,0:T(8,128)(2,1)} %pad.20.refs_1_, ...), custom_call_target="tpu_custom_call" | custom-call | tf_op jit(solution)/shard_map/pallas_call | solution.py:934
  268.5 0.8 constant_dynamic-slice_fusion.1
  269.2 0.6 slice_bitcast_fusion.2
  269.8 0.6 slice_bitcast_fusion.3
  270.4 0.7 slice_bitcast_fusion.1
  271.1 0.7 fusion.3
  271.8 0.6 fusion
  272.5 0.5 constant_dynamic-slice_fusion
  273.0 1.7 bitcast_convert_fusion
  274.7 0.0 copy-start.3
  274.7 2.8 copy.29
  277.5 0.0 copy-start.4
  277.6 0.0 copy-start.2
  277.6 0.0 copy-start.1
  277.6 1.1 copy.28
  278.7 0.0 copy-done.3
  278.7 0.7 copy.39
  279.4 0.0 copy-done.4
  279.4 0.6 copy.40
  280.0 0.0 copy-done.2
  280.0 0.7 copy.41
  280.7 0.0 copy-done.1
  280.7 0.7 copy.42
  (7 shorter events, 0.1 us)
Async XLA Ops:
  7.1 2.7 copy-start
  274.7 4.0 %copy-start.3 = (f32[32,1536]{1,0:T(8,128)S(1)}, f32[32,1536]{1,0:T(8,128)}, u32[]{:S(2)}) copy-start(f32[32,1536]{1,0:T(8,128)} %get-tuple-element.21) | copy-start | bytes 589828
  277.5 1.8 copy-start.4
  277.6 2.4 copy-start.2
  277.6 3.1 %copy-start.1 = (f32[128,512]{1,0:T(8,128)S(1)}, f32[128,512]{1,0:T(8,128)}, u32[]{:S(2)}) copy-start(f32[128,512]{1,0:T(8,128)} %get-tuple-element.24) | copy-start | bytes 786436
